TPU v7x, 32 devices: a whole 2x2x4 slice. The times are simulated.
32 devices in a mesh: local: 4 (over z), data: 8 (over y, x, core).
Axes of the slice: x: 2, y: 2, z: 4, core: 2. Of those that a mesh axis runs over, the one named last changes fastest.
Arguments:
- tokens: bfloat16 [32768, 1280], P(('data', 'local'))
- cotangent: bfloat16 [32768, 1280], P(('data', 'local'))
- w_up: bfloat16 [3, 1280, 5120], P(None, ('data', 'local'))
- w_down: bfloat16 [3, 5120, 1280], P(None, ('data', 'local'))
- lora_a: float32 [3, 1280, 4], replicated
- lora_b: float32 [3, 4, 5120], replicated
Outputs:
- output 1: bfloat16 [32768, 1280], P(('data', 'local'))
- output 2: bfloat16 [32768, 1280], P(('data', 'local'))
- output 3: float32 [3, 1280, 4], replicated
- output 4: float32 [3, 4, 5120], replicated
All inputs are finite; a program needn't handle non-finite values.
Results may differ from a plain program's by a relative error of at most 0.0163844.
Values are sent between devices in bfloat16 or wider.
A program may use at most 1 GiB of HBM per device.

v0:
```python
import jax
import jax.numpy as jnp
from jax import lax
from jax.sharding import PartitionSpec as P

GROUP = ("data", "local")
NORM_EPS = 1e-6
FULL_PRECISION = lax.Precision.HIGHEST


def gelu_tanh(pre_f):
    return jax.nn.gelu(pre_f, approximate=True)


def layer_forward(resid, full_up, full_down, adapt_a, adapt_b):
    resid_f = resid.astype(jnp.float32)
    inv_rms = lax.rsqrt(jnp.mean(resid_f * resid_f, axis=-1, keepdims=True) + NORM_EPS)
    normed = (resid_f * inv_rms).astype(jnp.bfloat16)
    low_rank = jnp.dot(normed, adapt_a, precision=FULL_PRECISION, preferred_element_type=jnp.float32)
    pre_act = (jnp.dot(normed, full_up, preferred_element_type=jnp.float32) + jnp.dot(low_rank, adapt_b, precision=FULL_PRECISION, preferred_element_type=jnp.float32)).astype(jnp.bfloat16)
    hidden_act = gelu_tanh(pre_act.astype(jnp.float32)).astype(jnp.bfloat16)
    new_resid = (resid_f + jnp.dot(hidden_act, full_down, preferred_element_type=jnp.float32)).astype(jnp.bfloat16)
    return new_resid, (resid, inv_rms, normed, low_rank, pre_act)


def layer_backward(d_resid, saved, full_up, full_down, adapt_a, adapt_b):
    resid, inv_rms, normed, low_rank, pre_act = saved
    d_hidden = jnp.einsum("th,fh->tf", d_resid, full_down, preferred_element_type=jnp.float32).astype(jnp.bfloat16)
    gelu_pull = jax.vjp(gelu_tanh, pre_act.astype(jnp.float32))[1]
    d_pre = gelu_pull(d_hidden.astype(jnp.float32))[0].astype(jnp.bfloat16)
    d_low = jnp.einsum("tf,rf->tr", d_pre, adapt_b, precision=FULL_PRECISION, preferred_element_type=jnp.float32)
    grad_b = jnp.einsum("tr,tf->rf", low_rank, d_pre, precision=FULL_PRECISION, preferred_element_type=jnp.float32)
    grad_a = jnp.einsum("th,tr->hr", normed, d_low, precision=FULL_PRECISION, preferred_element_type=jnp.float32)
    d_main = jnp.einsum("tf,hf->th", d_pre, full_up, preferred_element_type=jnp.float32).astype(jnp.bfloat16)
    d_side = jnp.einsum("tr,hr->th", d_low, adapt_a, precision=FULL_PRECISION, preferred_element_type=jnp.float32).astype(jnp.bfloat16)
    d_norm_f = (d_main + d_side).astype(jnp.float32)
    resid_f = resid.astype(jnp.float32)
    row_dot = jnp.mean(resid_f * d_norm_f, axis=-1, keepdims=True)
    d_resid_f = d_resid.astype(jnp.float32) + inv_rms * d_norm_f - resid_f * (inv_rms * inv_rms * inv_rms) * row_dot
    return d_resid_f.astype(jnp.bfloat16), grad_a, grad_b


def solution(mesh):
    data_size = mesh.shape["data"]
    tok_spec = P(GROUP, None)
    weight_spec = P(None, GROUP, None)

    def device_step(tokens, cotangent, up_shards, down_shards, value_a6, array_b6):
        local_idx = lax.axis_index("local")
        num_layers = up_shards.shape[0]
        up_rows = up_shards.shape[1] * data_size
        down_rows = down_shards.shape[1] * data_size
        resid = tokens
        kept = []
        for layer in range(num_layers):
            full_up = lax.all_gather(up_shards[layer], GROUP, axis=0, tiled=True)
            full_down = lax.all_gather(down_shards[layer], GROUP, axis=0, tiled=True)
            resid, saved = layer_forward(resid, full_up, full_down, value_a6[layer], array_b6[layer])
            keep_up = lax.dynamic_slice_in_dim(full_up, local_idx * up_rows, up_rows, axis=0)
            keep_down = lax.dynamic_slice_in_dim(full_down, local_idx * down_rows, down_rows, axis=0)
            kept.append((saved, keep_up, keep_down))
        d_resid = cotangent
        grads_a = []
        grads_b = []
        for layer in reversed(range(num_layers)):
            saved, keep_up, keep_down = kept[layer]
            full_up = lax.all_gather(keep_up, "local", axis=0, tiled=True)
            full_down = lax.all_gather(keep_down, "local", axis=0, tiled=True)
            d_resid, grad_a, grad_b = layer_backward(d_resid, saved, full_up, full_down, value_a6[layer], array_b6[layer])
            grad_a, grad_b = lax.psum((grad_a, grad_b), GROUP)
            grads_a.insert(0, grad_a)
            grads_b.insert(0, grad_b)
        return resid, d_resid, jnp.stack(grads_a), jnp.stack(grads_b)

    return jax.shard_map(device_step, mesh=mesh, in_specs=(tok_spec, tok_spec, weight_spec, weight_spec, P(), P()), out_specs=(tok_spec, tok_spec, P(), P()), check_vma=False)
```

profile of v0, /device:TPU:0, one launch (start us, length us, event | category | flops | bytes accessed | tf_op | source)
XLA Modules:
  0.0 2178.7 jit_solution(10890007912577680626)
XLA Ops:
  14.5 97.7 %all-gather.35.cloned.1.call-done = bf16[1,5120,1280]{2,1,0:T(8,128)(2,1)} async-done(((bf16[1,160,1280]{2,1,0:T(8,128)(2,1)}), bf16[1,5120,1280]{2,1,0:T(8,128)(2,1)}) %all-gather.35.cloned.1.call-update) | async-done | bytes 13107216 | tf_op jit(solution)/shard_map/all_gather | solution.py:57
  116.1 95.2 %all-gather.33.cloned.1.call-done = bf16[1,1280,5120]{2,1,0:T(8,128)(2,1)} async-done(((bf16[1,40,5120]{2,1,0:T(8,128)(2,1)}), bf16[1,1280,5120]{2,1,0:T(8,128)(2,1)}) %all-gather.33.cloned.1.call-update) | async-done | bytes 13107216 | tf_op jit(solution)/shard_map/all_gather | solution.py:56
  215.2 95.1 %all-gather.31.cloned.1.call-done = bf16[1,5120,1280]{2,1,0:T(8,128)(2,1)} async-done(((bf16[1,160,1280]{2,1,0:T(8,128)(2,1)}), bf16[1,5120,1280]{2,1,0:T(8,128)(2,1)}) %all-gather.31.cloned.1.call-update) | async-done | bytes 13107216 | tf_op jit(solution)/shard_map/all_gather | solution.py:57
  314.2 95.1 %all-gather.29.cloned.1.call-done = bf16[1,1280,5120]{2,1,0:T(8,128)(2,1)} async-done(((bf16[1,40,5120]{2,1,0:T(8,128)(2,1)}), bf16[1,1280,5120]{2,1,0:T(8,128)(2,1)}) %all-gather.29.cloned.1.call-update) | async-done | bytes 13107216 | tf_op jit(solution)/shard_map/all_gather | solution.py:56
  416.6 92.2 %all-gather.27.cloned.1.call-done = bf16[1,5120,1280]{2,1,0:T(8,128)(2,1)} async-done(((bf16[1,160,1280]{2,1,0:T(8,128)(2,1)}), bf16[1,5120,1280]{2,1,0:T(8,128)(2,1)}) %all-gather.27.cloned.1.call-update) | async-done | bytes 13107216 | tf_op jit(solution)/shard_map/all_gather | solution.py:57
  512.8 94.9 %all-gather.25.cloned.1.call-done = bf16[1,1280,5120]{2,1,0:T(8,128)(2,1)} async-done(((bf16[1,40,5120]{2,1,0:T(8,128)(2,1)}), bf16[1,1280,5120]{2,1,0:T(8,128)(2,1)}) %all-gather.25.cloned.1.call-update) | async-done | bytes 13107216 | tf_op jit(solution)/shard_map/all_gather | solution.py:56
  628.3 21.6 add_convert_fusion.2
  649.9 24.6 %fusion.89 = (f32[1024]{0:T(1024)S(1)}, bf16[1024,1280]{1,0:T(8,128)(2,1)S(1)}) fusion(bf16[1,5120,1280]{2,1,0:T(8,128)(2,1)} %all-gather.27.cloned.1.call-done, bf16[1024,5120]{1,0:T(8,128)(2,1)} %add_convert_fusion.2, bf16[1024,1280]{1,0:T(8,128)(2,1)S(1)} %copy-done), kind=kOutput, calls=%fused_computation.122 | convolution fusion | flops 13482064896 | bytes 28839936 | tf_op jit(solution)/shard_map/dot_general | solution.py:22
  698.1 21.9 %add_convert_fusion.1 = bf16[1024,5120]{1,0:T(8,128)(2,1)} fusion(f32[1024,5120]{1,0:T(8,128)} %fusion.51, f32[1024,4]{0,1:T(4,128)S(1)} %fusion.142, f32[3,4,5120]{2,1,0:T(4,128)S(1)} %copy-done.6), kind=kOutput, calls=%fused_computation.52 | convolution fusion | flops 262144000 | bytes 31555584 | tf_op jit(solution)/shard_map/dot_general | solution.py:20
  720.0 24.4 %fusion.94 = (f32[1024]{0:T(1024)S(1)}, bf16[1024,1280]{1,0:T(8,128)(2,1)S(1)}) fusion(bf16[1,5120,1280]{2,1,0:T(8,128)(2,1)} %all-gather.31.cloned.1.call-done, bf16[1024,5120]{1,0:T(8,128)(2,1)} %add_convert_fusion.1, bf16[1024,1280]{1,0:T(8,128)(2,1)S(1)} %get-tuple-element.23), kind=kOutput, calls=%fused_computation.127 | convolution fusion | flops 13482064896 | bytes 28839936 | tf_op jit(solution)/shard_map/dot_general | solution.py:22
  772.0 21.5 add_convert_fusion
  793.5 25.4 %fusion.96 = bf16[1024,1280]{1,0:T(8,128)(2,1)} fusion(bf16[1024,1280]{1,0:T(8,128)(2,1)S(1)} %get-tuple-element.25, bf16[1,5120,1280]{2,1,0:T(8,128)(2,1)} %all-gather.35.cloned.1.call-done, bf16[1024,5120]{1,0:T(8,128)(2,1)} %add_convert_fusion), kind=kOutput, calls=%fused_computation.129 | convolution fusion | flops 13478133760 | bytes 28835840 | tf_op jit(solution)/shard_map/dot_general | solution.py:22
  834.8 32.2 %fusion.11 = bf16[1024,5120]{1,0:T(8,128)(2,1)} fusion(bf16[1024,5120]{1,0:T(8,128)(2,1)} %add_convert_fusion, bf16[1024,1280]{1,0:T(8,128)(2,1)} %param.7, bf16[1,5120,1280]{2,1,0:T(8,128)(2,1)} %all-gather.37.cloned.1.call-done), kind=kOutput, calls=%fused_computation.28 | convolution fusion | flops 13542359040 | bytes 36700160 | tf_op jit(solution)/shard_map/th,fh->tf/dot_general | solution.py:28
  878.2 183.6 %all-gather.39.cloned.1.call-done = bf16[1,1280,5120]{2,1,0:T(8,128)(2,1)} async-done(((bf16[1,320,5120]{2,1,0:T(8,128)(2,1)}), bf16[1,1280,5120]{2,1,0:T(8,128)(2,1)}) %all-gather.39.cloned.1.call-update) | async-done | bytes 13107216 | tf_op jit(solution)/shard_map/all_gather | solution.py:67
  1061.8 21.0 fusion.111
  1093.6 195.2 %all-gather.41.cloned.1.call-done = bf16[1,5120,1280]{2,1,0:T(8,128)(2,1)} async-done(((bf16[1,1280,1280]{2,1,0:T(8,128)(2,1)}), bf16[1,5120,1280]{2,1,0:T(8,128)(2,1)}) %all-gather.41.cloned.1.call-update) | async-done | bytes 13107216 | tf_op jit(solution)/shard_map/all_gather | solution.py:68
  1288.9 32.0 %fusion.5 = bf16[1024,5120]{1,0:T(8,128)(2,1)} fusion(bf16[1024,5120]{1,0:T(8,128)(2,1)} %add_convert_fusion.1, bf16[1024,1280]{1,0:T(8,128)(2,1)} %fusion.77, bf16[1,5120,1280]{2,1,0:T(8,128)(2,1)} %all-gather.41.cloned.1.call-done), kind=kOutput, calls=%fused_computation.22 | convolution fusion | flops 13542359040 | bytes 36700160 | tf_op jit(solution)/shard_map/th,fh->tf/dot_general | solution.py:28
  1332.1 183.7 %all-gather.43.cloned.1.call-done = bf16[1,1280,5120]{2,1,0:T(8,128)(2,1)} async-done(((bf16[1,320,5120]{2,1,0:T(8,128)(2,1)}), bf16[1,1280,5120]{2,1,0:T(8,128)(2,1)}) %all-gather.43.cloned.1.call-update) | async-done | bytes 13107216 | tf_op jit(solution)/shard_map/all_gather | solution.py:67
  1551.8 191.0 %all-gather.45.cloned.1.call-done = bf16[1,5120,1280]{2,1,0:T(8,128)(2,1)} async-done(((bf16[1,1280,1280]{2,1,0:T(8,128)(2,1)}), bf16[1,5120,1280]{2,1,0:T(8,128)(2,1)}) %all-gather.45.cloned.1.call-update) | async-done | bytes 13107216 | tf_op jit(solution)/shard_map/all_gather | solution.py:68
  1742.9 32.0 %fusion.8 = bf16[1024,5120]{1,0:T(8,128)(2,1)} fusion(bf16[1024,5120]{1,0:T(8,128)(2,1)} %add_convert_fusion.2, bf16[1024,1280]{1,0:T(8,128)(2,1)} %fusion.80, bf16[1,5120,1280]{2,1,0:T(8,128)(2,1)} %all-gather.45.cloned.1.call-done), kind=kOutput, calls=%fused_computation.25 | convolution fusion | flops 13542359040 | bytes 36700160 | tf_op jit(solution)/shard_map/th,fh->tf/dot_general | solution.py:28
  1804.6 165.2 %all-gather.47.cloned.1.call-done = bf16[1,1280,5120]{2,1,0:T(8,128)(2,1)} async-done(((bf16[1,320,5120]{2,1,0:T(8,128)(2,1)}), bf16[1,1280,5120]{2,1,0:T(8,128)(2,1)}) %all-gather.47.cloned.1.call-update) | async-done | bytes 13107216 | tf_op jit(solution)/shard_map/all_gather | solution.py:67
  1969.8 21.0 fusion.117
  2001.8 39.3 %all-reduce = (f32[1,1280,4]{1,2,0:T(4,128)S(1)}, f32[1,1280,4]{1,2,0:T(4,128)S(1)}, f32[1,1280,4]{1,2,0:T(4,128)S(1)}) all-reduce(f32[1,1280,4]{1,2,0:T(4,128)S(1)} %copy-done.15, f32[1,1280,4]{1,2,0:T(4,128)S(1)} %copy-done.16, f32[1,1280,4]{1,2,0:T(4,128)S(1)} %convolution_bitcast_fusion.5), channel_id=1, replica_groups=mesh['local'=4,'data'=8] {'data','local'}, use_global_device_ids=true, to_apply=%region_8.0 | all-reduce | flops 15360 | bytes 122880 | tf_op jit(solution)/shard_map/psum | solution.py:70
  2041.8 128.4 %all-reduce.4.cloned.1.call-done = (f32[1,4,5120]{2,1,0:T(4,128)}, f32[1,4,5120]{2,1,0:T(4,128)}, f32[1,4,5120]{2,1,0:T(4,128)}) async-done(((f32[1,4,5120]{2,1,0:T(4,128)}, f32[1,4,5120]{2,1,0:T(4,128)}, f32[1,4,5120]{2,1,0:T(4,128)}), (f32[1,4,5120]{2,1,0:T(4,128)}, f32[1,4,5120]{2,1,0:T(4,128)}, f32[1,4,5120]{2,1,0:T(4,128)})) %all-reduce.4.cloned.1.call-update) | async-done | bytes 245776 | tf_op jit(solution)/shard_map/psum | solution.py:70
  (128 shorter events, 229.9 us)
Async XLA Ops:
  7.2 105.0 %all-gather.35.cloned.1.call-start = ((), (), s32[]{:S(2)}) async-start(), calls=%async_computation.5 | async-start | bytes 13516800 | tf_op jit(solution)/shard_map/all_gather | solution.py:57
  9.6 201.7 %all-gather.33.cloned.1.call-start = ((), (), s32[]{:S(2)}) async-start(), calls=%async_computation.4 | async-start | bytes 13516800 | tf_op jit(solution)/shard_map/all_gather | solution.py:56
  11.9 298.4 %all-gather.31.cloned.1.call-start = ((), (), s32[]{:S(2)}) async-start(), calls=%async_computation.3 | async-start | bytes 13516800 | tf_op jit(solution)/shard_map/all_gather | solution.py:57
  12.7 396.6 %all-gather.29.cloned.1.call-start = ((), (), s32[]{:S(2)}) async-start(), calls=%async_computation.2 | async-start | bytes 13516800 | tf_op jit(solution)/shard_map/all_gather | solution.py:56
  13.2 495.5 %all-gather.27.cloned.1.call-start = ((), (), s32[]{:S(2)}) async-start(), calls=%async_computation.1 | async-start | bytes 13516800 | tf_op jit(solution)/shard_map/all_gather | solution.py:57
  13.8 593.8 %all-gather.25.cloned.1.call-start = ((), (), s32[]{:S(2)}) async-start(), calls=%async_computation | async-start | bytes 13516800 | tf_op jit(solution)/shard_map/all_gather | solution.py:56
  14.4 820.3 %all-gather.37.cloned.1.call-start = ((), (), s32[]{:S(2)}) async-start(), calls=%async_computation.6 | async-start | bytes 16384000 | tf_op jit(solution)/shard_map/all_gather | solution.py:68
  116.0 945.8 %all-gather.39.cloned.1.call-start = ((), (), s32[]{:S(2)}) async-start(), calls=%async_computation.7 | async-start | bytes 16384000 | tf_op jit(solution)/shard_map/all_gather | solution.py:67
  215.2 198.0 %copy-start = (bf16[1024,1280]{1,0:T(8,128)(2,1)S(1)}, bf16[1024,1280]{1,0:T(8,128)(2,1)}, u32[]{:S(2)}) copy-start(bf16[1024,1280]{1,0:T(8,128)(2,1)} %param.6) | copy-start | bytes 7864324
  215.2 199.2 %copy-start.13 = (f32[3,1280,4]{1,2,0:T(4,128)S(1)}, f32[3,1280,4]{1,2,0:T(4,128)}, u32[]{:S(2)}) copy-start(f32[3,1280,4]{1,2,0:T(4,128)} %param.10) | copy-start | bytes 184324
  215.2 1073.7 %all-gather.41.cloned.1.call-start = ((), (), s32[]{:S(2)}) async-start(), calls=%async_computation.8 | async-start | bytes 16384000 | tf_op jit(solution)/shard_map/all_gather | solution.py:68
  314.1 1201.7 %all-gather.43.cloned.1.call-start = ((), (), s32[]{:S(2)}) async-start(), calls=%async_computation.9 | async-start | bytes 16384000 | tf_op jit(solution)/shard_map/all_gather | solution.py:67
  413.1 1329.7 %all-gather.45.cloned.1.call-start = ((), (), s32[]{:S(2)}) async-start(), calls=%async_computation.10 | async-start | bytes 16384000 | tf_op jit(solution)/shard_map/all_gather | solution.py:68
  414.4 213.9 %copy-start.17 = (f32[1024]{0:T(1024)}, f32[1024]{0:T(1024)S(1)}, u32[]{:S(2)}) copy-start(f32[1024]{0:T(1024)S(1)} %get-tuple-element.17) | copy-start | bytes 12292
  416.6 211.8 %copy-start.7 = (f32[1024,4]{0,1:T(4,128)}, f32[1024,4]{0,1:T(4,128)S(1)}, u32[]{:S(2)}) copy-start(f32[1024,4]{0,1:T(4,128)S(1)} %fusion.145) | copy-start | bytes 49156
  512.5 115.8 %copy-start.6 = (f32[3,4,5120]{2,1,0:T(4,128)S(1)}, f32[3,4,5120]{2,1,0:T(4,128)}, u32[]{:S(2)}) copy-start(f32[3,4,5120]{2,1,0:T(4,128)} %param.11) | copy-start | bytes 737284
  512.5 1457.2 %all-gather.47.cloned.1.call-start = ((), (), s32[]{:S(2)}) async-start(), calls=%async_computation.11 | async-start | bytes 16384000 | tf_op jit(solution)/shard_map/all_gather | solution.py:67
  674.5 45.5 %copy-start.2 = (bf16[1024,1280]{1,0:T(8,128)(2,1)}, bf16[1024,1280]{1,0:T(8,128)(2,1)S(1)}, u32[]{:S(2)}) copy-start(bf16[1024,1280]{1,0:T(8,128)(2,1)S(1)} %get-tuple-element.23) | copy-start | bytes 7864324
  744.4 345.1 %copy-start.4 = (bf16[1024,1280]{1,0:T(8,128)(2,1)}, bf16[1024,1280]{1,0:T(8,128)(2,1)S(1)}, u32[]{:S(2)}) copy-start(bf16[1024,1280]{1,0:T(8,128)(2,1)S(1)} %get-tuple-element.25) | copy-start | bytes 7864324
  793.5 1376.7 %all-reduce.4.cloned.1.call-start = ((), (), s32[]{:S(2)}) async-start(), calls=%async_computation.12 | async-start | bytes 491520 | tf_op jit(solution)/shard_map/psum | solution.py:70
  878.2 204.7 %copy-start.14 = (f32[3,1280,4]{1,2,0:T(4,128)S(1)}, f32[3,1280,4]{1,2,0:T(4,128)}, u32[]{:S(2)}) copy-start(f32[3,1280,4]{1,2,0:T(4,128)} %param.10) | copy-start | bytes 184324
  878.2 211.3 %copy-start.23 = (f32[1024]{0:T(1024)S(1)}, f32[1024]{0:T(1024)}, u32[]{:S(2)}) copy-start(f32[1024]{0:T(1024)} %get-tuple-element.20) | copy-start | bytes 12292
  1332.1 204.8 %copy-start.3 = (bf16[1024,1280]{1,0:T(8,128)(2,1)S(1)}, bf16[1024,1280]{1,0:T(8,128)(2,1)}, u32[]{:S(2)}) copy-start(bf16[1024,1280]{1,0:T(8,128)(2,1)} %copy-done.2) | copy-start | bytes 7864324
  1804.6 193.1 %copy-start.21 = (f32[1024]{0:T(1024)S(1)}, f32[1024]{0:T(1024)}, u32[]{:S(2)}) copy-start(f32[1024]{0:T(1024)} %get-tuple-element.16) | copy-start | bytes 12292
  (19 other events, 251.5 us)
Sparse Core Ops, SparseCore 0:
  11.4 100.7 all-gather.34
  115.0 96.1 all-gather.32
  214.1 96.1 all-gather.30
  313.0 96.1 all-gather.28
  412.5 96.1 all-gather.26
  511.4 96.1 all-gather.24
  609.2 225.4 all-gather.36
  836.3 225.4 all-gather.38
  1063.4 225.4 all-gather.40
  1290.3 225.4 all-gather.42
  1517.4 225.4 all-gather.44
  1744.3 225.4 all-gather.46
  2041.3 128.8 all-reduce.3
where the time goes:
time: 2180 us
  waiting for transfers between devices  1640 us (75%)
  matrix products  445 us (20%)
  blocking collectives  39.3 us (2%)
  local copies, waits for them, and re-layouts  27.8 us (1%)
    all_gather x3, waiting for transfers between devices, device_step(): full_up = lax.all_gather(keep_up, 'local', axis=0, tiled=True)  533 us
    all_gather x3, waiting for transfers between devices, device_step(): full_down = lax.all_gather(keep_down, 'local', axis=0, tiled=True)  402 us
    all_gather x3, waiting for transfers between devices, device_step(): full_up = lax.all_gather(up_shards[layer], GROUP, axis=0, tiled=True)  285 us
    all_gather x3, waiting for transfers between devices, device_step(): full_down = lax.all_gather(down_shards[layer], GROUP, axis=0, tiled=True)  285 us
    psum x1, waiting for transfers between devices, device_step(): grad_a, grad_b = lax.psum((grad_a, grad_b), GROUP)  128 us
    dot_general x3, matrix products, layer_backward(): jnp.einsum('th,fh->tf', d_resid, full_down, preferred_element_type=jnp.fl...  96.2 us
    dot_general x3, matrix products, layer_forward(): jnp.dot(hidden_act, full_down, preferred_element_type=jnp.float32)  74.5 us
    dot_general x3, matrix products, layer_forward(): jnp.dot(low_rank, adapt_b, precision=FULL_PRECISION, preferred_element_ty...  64.9 us
  transfers between devices with their start and end apart: 13, of which 13 were waited for; matrix products, arithmetic and copies ran while one was open for 21% of the time, Pallas kernels for 0%

commit v1 on v0

v1 whole, which is shorter than its diff:
```python
import math

import jax
import jax.numpy as jnp
from jax import lax
from jax.experimental import pallas as pl
from jax.experimental.pallas import tpu as pltpu
from jax.sharding import PartitionSpec as P

GROUP = ("data", "local")
MESH = pl.DeviceIdType.MESH
BF16, F32 = jnp.bfloat16, jnp.float32
ROWS = 512
LANES = 128
NORM_EPS = 1e-6
GELU_S = math.sqrt(2.0 / math.pi)
GELU_C = 0.044715

LAYERS, TOKENS, HIDDEN, FF, RANK = 3, 1024, 1280, 5120, 4
NT = 10
TILES = 2 * LAYERS * NT
UP_ROWS, DOWN_ROWS = HIDDEN // 32, FF // 32
UP_TILE, DOWN_TILE = FF // NT, DOWN_ROWS // NT
OUT_COLS = 256
QUARTER = FF // 4
RING, SRING = 20, 16
OFFSETS = (7, 6, 5, 4, 3, 2, 1, 0, -1)
LEAD = OFFSETS[0]
FUSED_FROM = 5 * NT
SUB = 256
SUBS = QUARTER // SUB
G_COLS = 3328
G_HALF = G_COLS // 2
G_EDGE = (FF + HIDDEN) // 2
G_STAGES = 6
SPLITS = (((0, 424), (424, 424), (848, 432)), ((0, 88), (88, 88), (176, 80)))


def dot(a, b):
    return jnp.dot(a, b, preferred_element_type=F32)


def dot_t(a, b):
    return lax.dot_general(a, b, (((1,), (1,)), ((), ())), preferred_element_type=F32)


def split3(x):
    hi = x.astype(BF16).astype(F32)
    rest = x - hi
    mid = rest.astype(BF16).astype(F32)
    return hi, mid, (rest - mid).astype(BF16).astype(F32)


def stack_left(x):
    hi, mid, lo = split3(x)
    return hi, hi, hi, mid, mid, lo


def stack_right(x):
    hi, mid, lo = split3(x)
    return hi, mid, lo, hi, mid, hi


def sum3(x):
    return x[0:8] + x[8:16] + x[16:24]


def gelu_inner(x):
    x2 = x * x
    return x2, jnp.tanh(x * (GELU_S + (GELU_S * GELU_C) * x2))


def step_kernel(
    tokens, cotangent, w_up, w_down, adapt_a, adapt_b,
    out_tokens, grad_tokens, grad_a, grad_b,
    land_up, land_down, back_up, back_down, pre_acts, resids, normeds,
    own_up, own_down, x, u, d, inv_s, b6, a6, v6, v3, dlow, gb, send_g, half_g, recv_first, recv_half, recv_last,
    recv_sem, pair_sem, send_sem, back_recv, back_send, swap_recv, swap_send, g_recv, g_send, load_sem, back_sem, w_sem, act_sem, keep_sem, credit,
):
    z = lax.axis_index("local")
    dev = lax.axis_index("data")
    core = lax.rem(dev, 2)
    dx = dev + 2 - 4 * lax.rem(dev // 2, 2)
    dy = dev + 4 - 8 * (dev // 4)
    dd = dx + dy - dev
    dc = dev + 1 - 2 * core
    zp = z + 1 - 2 * lax.rem(z, 2)
    za, zb = 3 - z, 3 - zp
    parity = lax.rem(lax.rem(dev // 2, 2) + dev // 4 + z, 2)
    is_end = jnp.logical_or(z == 0, z == 3)
    is_mid = jnp.logical_not(is_end)
    to_p, to_a, to_b = (zp, dev), (za, dev), (zb, dev)
    to_x, to_y, to_c = (z, dx), (z, dy), (z, dc)
    cols = (dev, dx, dy, dd)
    pair_cols = (dc, dc + dx - dev, dc + dy - dev, dc + dd - dev)

    def remote(src, dst, ssem, rsem, target):
        return pltpu.make_async_remote_copy(src, dst, ssem, rsem, device_id=target, device_id_type=MESH)

    def both(cond, on, off):
        pl.when(cond)(on)
        pl.when(jnp.logical_not(cond))(off)

    loads = [
        pltpu.make_async_copy(w_up, own_up, load_sem.at[0]),
        pltpu.make_async_copy(w_down, own_down, load_sem.at[1]),
        pltpu.make_async_copy(tokens, x, load_sem.at[2]),
        pltpu.make_async_copy(cotangent, d, load_sem.at[3]),
    ]
    for load in loads:
        load.start()
    barrier = pltpu.get_barrier_semaphore()
    for target in (to_p, to_x, to_y, to_c, to_b):
        pl.semaphore_signal(barrier, inc=1, device_id=target, device_id_type=MESH)

    @pl.when(is_mid)
    def _():
        pl.semaphore_signal(barrier, inc=1, device_id=to_a, device_id_type=MESH)
        pl.semaphore_wait(barrier, 6)

    @pl.when(is_end)
    def _():
        pl.semaphore_wait(barrier, 5)

    loads[0].wait()
    loads[1].wait()

    def is_up(k):
        m = k // NT
        return jnp.logical_or(jnp.logical_and(lax.rem(m, 2) == 0, m < 4), m == 5)

    def slab(up, k, col, zz, own=False):
        layer, t, n = k // (2 * NT), lax.rem(k, NT), 4 * col + zz
        slot = lax.rem(layer, 2)
        if up:
            c = pl.ds(pl.multiple_of(UP_TILE * t, LANES), UP_TILE)
            return own_up.at[layer, :, c] if own else land_up.at[slot, pl.ds(pl.multiple_of(UP_ROWS * n, 8), UP_ROWS), c]
        r = pl.multiple_of(DOWN_TILE * t, 16)
        return own_down.at[layer, pl.ds(r, DOWN_TILE), :] if own else land_down.at[slot, pl.ds(pl.multiple_of(DOWN_ROWS * n + r, 16), DOWN_TILE), :]

    def send(up, k, entry):
        rel, zz, target, to_rel = entry
        own = rel == own_c and zz is z
        index = [e is entry for e in order].index(True)
        return remote(slab(up, k, cols[rel], zz, own), slab(up, k, cols[rel], zz), send_sem.at[lax.rem(k, SRING), index],
                      recv_sem.at[lax.rem(k, RING), to_rel * 4 + zz], target)

    def wait_slab(up, k, rel, zz):
        s = slab(up, k, cols[rel], zz)
        remote(s, s, send_sem.at[0, 0], recv_sem.at[lax.rem(k, RING), rel * 4 + zz], to_x).wait_recv()

    def pair_copy(up, k, g, c):
        layer, t = k // (2 * NT), lax.rem(k, NT)
        slot = lax.rem(layer, 2)
        if up:
            s = land_up.at[slot, pl.ds(pl.multiple_of(4 * UP_ROWS * c, 8), 4 * UP_ROWS), pl.ds(pl.multiple_of(UP_TILE * t, LANES), UP_TILE)]
        else:
            s = land_down.reshape(2, 32, DOWN_ROWS, HIDDEN).at[slot, pl.ds(4 * c, 4), pl.ds(pl.multiple_of(DOWN_TILE * t, 16), DOWN_TILE), :]
        return remote(s, s, send_sem.at[lax.rem(k, SRING), len(order) + 1 + g], pair_sem.at[lax.rem(k, RING), g], to_c)

    own_c, x_c, y_c, diag_c = range(4)
    own_sends = [(own_c, z, to_p, own_c), (own_c, z, to_a, own_c), (own_c, z, to_x, x_c), (own_c, z, to_y, y_c)]
    hop_p = [(own_c, zp, to_x, x_c), (own_c, zp, to_y, y_c), (own_c, zp, to_a, own_c)]
    hop_a = [(own_c, za, to_p, own_c), (own_c, za, to_x, x_c), (own_c, za, to_y, y_c)]
    hop_b = [(own_c, zb, to_p, own_c), (own_c, zb, to_x, x_c), (own_c, zb, to_y, y_c)]
    diag = [(y_c, z, to_x, diag_c), (x_c, zb, to_y, diag_c)]
    swap = [(diag_c, z, to_p, diag_c), (diag_c, zb, to_p, diag_c)]
    order = own_sends + hop_p + hop_a + hop_b + diag + swap

    def each(up, k, entries, act):
        for entry in entries:
            rel, zz, target, _ = entry
            if target is to_a or (target is to_p and rel == own_c and zz is not z):
                @pl.when(is_mid)
                def _():
                    act(send(up, k, entry))
            else:
                act(send(up, k, entry))

    def start(up, k, entries):
        each(up, k, entries, lambda copy: copy.start())

    def own_local(up, k):
        return pltpu.make_async_copy(slab(up, k, dev, z, True), slab(up, k, dev, z), send_sem.at[lax.rem(k, SRING), len(order)])

    def stage_own(up, k):
        start(up, k, own_sends)
        own_local(up, k).start()

    def stage_1(up, k):
        wait_slab(up, k, own_c, zp)
        start(up, k, hop_p)

        @pl.when(is_mid)
        def _():
            wait_slab(up, k, own_c, za)
            start(up, k, hop_a)

    def stage_2(up, k):
        wait_slab(up, k, own_c, zb)
        start(up, k, hop_b)

    def stage_3(up, k):
        @pl.when(is_end)
        def _():
            wait_slab(up, k, own_c, za)
            start(up, k, hop_a[1:])

    def stage_diag(up, k):
        wait_slab(up, k, y_c, z)
        start(up, k, diag[:1])
        wait_slab(up, k, x_c, zb)
        start(up, k, diag[1:])

    def stage_swap(up, k):
        wait_slab(up, k, diag_c, z)
        start(up, k, swap[:1])
        wait_slab(up, k, diag_c, zb)
        start(up, k, swap[1:])

    def stage_pair(up, k):
        own_local(up, k).wait()
        pair_copy(up, k, own_c, dev).start()
        for zz in (z, zp, za):
            wait_slab(up, k, x_c, zz)
        pair_copy(up, k, x_c, dx).start()
        for zz in (zp, za, zb):
            wait_slab(up, k, y_c, zz)
        pair_copy(up, k, y_c, dy).start()
        for zz in (zp, za):
            wait_slab(up, k, diag_c, zz)
        pair_copy(up, k, diag_c, dd).start()

    def stage_done(up, k):
        for g in range(4):
            pair_copy(up, k, g, pair_cols[g]).wait_recv()

    def stage_sent(up, k):
        each(up, k, order, lambda copy: copy.wait_send())
        for g in range(4):
            pair_copy(up, k, g, cols[g]).wait_send()

    stages = list(zip(OFFSETS[::-1], (stage_sent, stage_done, stage_pair, stage_swap, stage_diag, stage_3, stage_2, stage_1, stage_own)))

    def gather_step(i):
        for offset, stage in stages:
            k = i + offset

            @pl.when(jnp.logical_and(k >= 0, k < TILES))
            def _():
                both(is_up(k), lambda: stage(True, k), lambda: stage(False, k))

    def give_credits():
        for target in (to_p, to_x, to_y, to_c):
            pl.semaphore_signal(credit, inc=1, device_id=target, device_id_type=MESH)

        @pl.when(is_mid)
        def _():
            pl.semaphore_signal(credit, inc=1, device_id=to_a, device_id_type=MESH)

    def wait_credits():
        @pl.when(is_mid)
        def _():
            pl.semaphore_wait(credit, 5)

        @pl.when(is_end)
        def _():
            pl.semaphore_wait(credit, 4)

    quarter = 2 * parity + core

    def back_ref(matrix, layer, slot, sub, part=None):
        c = pl.ds(pl.multiple_of(SUB * sub, SUB), SUB)
        if matrix == 0:
            return back_up.at[layer, slot, :, c] if part is None else back_up.at[layer, slot, pl.ds(*part), c]
        if part is None:
            return back_down.at[layer, slot, c, :]
        return back_down.at[layer, slot, pl.ds(pl.multiple_of(SUB * sub + part[0], 8), part[1]), :]

    def back_copy(matrix, layer, sub, axis):
        part = SPLITS[matrix][axis]
        return remote(back_ref(matrix, layer, 0, sub, part), back_ref(matrix, layer, 2, sub, part), back_send.at[matrix, layer, sub, axis],
                      back_recv.at[matrix, layer, sub, axis], (to_x, to_y, to_p)[axis])

    def send_back(h):
        layer, sub = (LAYERS - 2) - h // (2 * SUBS), lax.rem(h, 2 * SUBS) // 2
        for matrix in range(2):
            @pl.when(lax.rem(h, 2) == matrix)
            def _():
                for axis in range(3):
                    back_copy(matrix, layer, sub, axis).start()

    def swap_own(layer, matrix):
        ref = (back_up, back_down)[matrix]
        return remote(ref.at[layer, 0], ref.at[layer, 1], swap_send.at[matrix, layer, SUBS], swap_recv.at[matrix, layer, SUBS], to_c)

    def swap_sub(matrix, layer, sub):
        return remote(back_ref(matrix, layer, 2, sub), back_ref(matrix, layer, 3, sub), swap_send.at[matrix, layer, sub], swap_recv.at[matrix, layer, sub], to_c)

    def g_copy(layer, stage):
        half = lambda c: pl.ds(pl.multiple_of(G_HALF * c, LANES), G_HALF)
        if stage == 0:
            src, dst, target = send_g.at[layer, :, half(1 - core)], recv_first.at[layer], to_c
        elif stage == 5:
            src, dst, target = half_g.at[layer, 4], recv_last.at[layer], to_c
        else:
            src, dst, target = half_g.at[layer, stage - 1], recv_half.at[layer, stage - 1], (to_x, to_y, to_p, to_b)[stage - 1]
        return remote(src, dst, g_send.at[layer, stage], g_recv.at[layer, stage], target)

    def g_step(layer, stage):
        if stage > 0:
            g_copy(layer, stage - 1).wait()
        if stage == 1:
            half_g[layer, 0] = send_g[layer, :, pl.ds(pl.multiple_of(G_HALF * core, LANES), G_HALF)] + recv_first[layer]
        elif 1 < stage < 6:
            half_g[layer, stage - 1] = half_g[layer, stage - 2] + recv_half[layer, stage - 2]
        if stage < 6:
            g_copy(layer, stage).start()

    def g_finish(layer):
        send_g[layer, :, pl.ds(pl.multiple_of(G_HALF * core, LANES), G_HALF)] = half_g[layer, 4]
        send_g[layer, :, pl.ds(pl.multiple_of(G_HALF * (1 - core), LANES), G_HALF)] = recv_last[layer]
        total = send_g[layer]
        grad_b[layer, :, 0:G_EDGE] = total[0:RANK, 0:G_EDGE]
        grad_b[layer, :, G_EDGE:FF] = total[RANK:2 * RANK, 0:FF - G_EDGE]
        grad_a[layer, :, :] = total[RANK:2 * RANK, FF - G_EDGE:G_EDGE]

    def write_blocks(ref, blocks):
        for i in range(3):
            ref[16 * i:16 * i + 16, :] = jnp.concatenate([blocks[2 * i], blocks[2 * i + 1]], axis=0).astype(BF16)

    def rows8(value):
        return jnp.concatenate([value, jnp.zeros_like(value)], axis=0)

    def adapters(layer):
        for c in range(0, FF, HIDDEN):
            write_blocks(b6.at[:, c:c + HIDDEN], stack_right(rows8(adapt_b[layer, :, c:c + HIDDEN])))
        write_blocks(a6, stack_right(rows8(adapt_a[layer])))

    def normalize(layer, save):
        @pl.loop(0, TOKENS // LANES)
        def _(i):
            r = pl.ds(pl.multiple_of(i * LANES, LANES), LANES)
            xf = x[r, :].astype(F32)
            inv = lax.rsqrt(jnp.mean(xf * xf, axis=-1, keepdims=True) + NORM_EPS)
            u[r, :] = (xf * inv).astype(BF16)
            inv_s[layer, r, :] = jnp.broadcast_to(inv, (LANES, LANES))

        adapters(layer)
        low = sum3(dot_t(a6[0:32, :], u[...]))
        left = stack_left(low)
        v3[layer, :, :] = jnp.concatenate([left[0], left[3], left[5]], axis=0)
        wide = jnp.concatenate(list(left) + [jnp.zeros((80, TOKENS), F32)], axis=0)
        v6[...] = jnp.transpose(wide).astype(BF16)
        if save:
            save_x(layer).start()
            save_u(layer).start()

    def save_x(layer):
        return pltpu.make_async_copy(x, resids.at[layer], load_sem.at[4])

    def save_u(layer):
        return pltpu.make_async_copy(u, normeds.at[layer], load_sem.at[5])

    def first_load(layer, t, buf):
        return pltpu.make_async_copy(land_up.at[lax.rem(layer, 2), :, pl.ds(pl.multiple_of(UP_TILE * t, LANES), UP_TILE)], buf.at[lax.rem(t, 2)], w_sem.at[0, lax.rem(t, 2)])

    def act_store(layer, t, acts):
        return pltpu.make_async_copy(acts.at[lax.rem(t, 2)], pre_acts.at[layer, :, pl.ds(pl.multiple_of(UP_TILE * t, LANES), UP_TILE)], act_sem.at[lax.rem(t, 2)])

    def keep_half(layer, t, h, buf):
        block = 2 * t + h - 5 * quarter
        copy = pltpu.make_async_copy(buf.at[lax.rem(t, 2), :, 256 * h:256 * h + 256],
                                     back_up.at[layer, 0, :, pl.ds(pl.multiple_of(256 * jnp.clip(block, 0, 4), LANES), 256)], keep_sem.at[h])
        return jnp.logical_and(block >= 0, block < 5), copy

    def first_product(layer, t, buf, acts, s):
        first_load(layer, t, buf).wait()
        for h in range(2):
            cond, copy = keep_half(layer, t, h, buf)
            pl.when(cond)(copy.start)

        @pl.when(t >= 2)
        def _():
            act_store(layer, t - 2, acts).wait()

        c = pl.ds(pl.multiple_of(UP_TILE * t, LANES), UP_TILE)
        pre = dot(u[...], buf[lax.rem(t, 2)]) + dot(v6[...], b6[:, c])
        act = pre.astype(BF16)
        acts[lax.rem(t, 2)] = act
        af = act.astype(F32)
        _, th = gelu_inner(af)
        half = 0.5 * af
        s[:, c] = (half + half * th).astype(BF16)
        act_store(layer, t, acts).start()
        for h in range(2):
            cond, copy = keep_half(layer, t, h, buf)
            pl.when(cond)(copy.wait)

    def second_load(layer, c, buf):
        return pltpu.make_async_copy(land_down.at[lax.rem(layer, 2), :, pl.ds(pl.multiple_of(OUT_COLS * c, LANES), OUT_COLS)], buf.at[lax.rem(c, 2)], w_sem.at[1, lax.rem(c, 2)])

    def second_keep(layer, c, buf):
        cc = pl.ds(pl.multiple_of(OUT_COLS * c, LANES), OUT_COLS)
        return pltpu.make_async_copy(buf.at[lax.rem(c, 2), pl.ds(pl.multiple_of(QUARTER * quarter, 16), QUARTER), :], back_down.at[layer, 0, :, cc], keep_sem.at[2])

    def second_product(layer, c, buf, s):
        second_load(layer, c, buf).wait()
        keep = second_keep(layer, c, buf)
        keep.start()
        cc = pl.ds(pl.multiple_of(OUT_COLS * c, LANES), OUT_COLS)
        x[:, cc] = (x[:, cc].astype(F32) + dot(s[...], buf[lax.rem(c, 2)])).astype(BF16)
        keep.wait()

    def gelu_both(act):
        af = act.astype(F32)
        x2, th = gelu_inner(af)
        half = 0.5 * af
        slope = 0.5 + 0.5 * th + half * (1.0 - th * th) * (GELU_S + (3.0 * GELU_S * GELU_C) * x2)
        return half + half * th, slope

    def low_parts(layer, dpre, c):
        cc = pl.ds(c, dpre.shape[1])
        dlow[...] += sum3(dot_t(b6[0:32, cc], dpre))
        gb[:, cc] = sum3(dot(v3[layer].astype(BF16), dpre))

    def close_layer(layer, acc):
        left = stack_left(dlow[...])
        wide = jnp.concatenate(list(left) + [jnp.zeros((80, TOKENS), F32)], axis=0)
        v6[...] = jnp.transpose(wide).astype(BF16)
        narrow = jnp.concatenate([left[0], left[3], left[5]], axis=0).astype(BF16)
        ga = sum3(dot(narrow, u[...]))
        send_g[layer, 0:RANK, 0:G_EDGE] = gb[0:RANK, 0:G_EDGE]
        send_g[layer, RANK:2 * RANK, 0:FF - G_EDGE] = gb[0:RANK, G_EDGE:FF]
        send_g[layer, RANK:2 * RANK, FF - G_EDGE:G_EDGE] = ga[0:RANK]
        send_g[layer, :, G_EDGE:G_COLS] = jnp.zeros((8, G_COLS - G_EDGE), F32)
        g_step(layer, 0)

        @pl.loop(0, TOKENS // LANES)
        def _(i):
            r = pl.ds(pl.multiple_of(i * LANES, LANES), LANES)
            side = dot(v6[r, :], a6[...]).astype(BF16)
            dn = (acc[r, :].astype(BF16) + side).astype(F32)
            xf = x[r, :].astype(F32)
            inv = inv_s[layer, r, 0:1]
            row = jnp.mean(xf * dn, axis=-1, keepdims=True)
            d[r, :] = (d[r, :].astype(F32) + inv * dn - xf * (inv * inv * inv * row)).astype(BF16)

    zero128 = jnp.zeros((80, HIDDEN), BF16)
    a6[48:LANES, :] = zero128
    for c in range(0, FF, HIDDEN):
        b6[48:LANES, c:c + HIDDEN] = zero128

    def forward(buf_a, buf_b, s, acts):
        def iteration(j, carry):
            i = j - LEAD

            pl.when(i == 2 * 2 * NT - LEAD)(wait_credits)
            gather_step(i)

            @pl.when(i == -2)
            def _():
                loads[2].wait()
                normalize(0, True)

            second = i >= 2 * NT + 4
            layer = jnp.where(second, 1, 0)
            lo = jnp.where(second, 2 * NT + 5, 1)

            @pl.when(jnp.logical_and(i >= lo - 1, i < lo - 1 + NT))
            def _():
                first_load(layer, i - lo + 1, buf_a).start()

            @pl.when(jnp.logical_and(i >= lo, i < lo + NT))
            def _():
                first_product(layer, i - lo, buf_a, acts, s)

            @pl.when(i == lo + NT)
            def _():
                act_store(layer, NT - 2, acts).wait()
                act_store(layer, NT - 1, acts).wait()

            pieces = HIDDEN // OUT_COLS
            prev = jnp.where(i >= 4 * NT - 1, 1, 0)
            lo2 = 2 * NT + 2 * NT * prev

            @pl.when(jnp.logical_and(i >= lo2 - 1, i < lo2 - 1 + pieces))
            def _():
                second_load(prev, i - lo2 + 1, buf_b).start()

            @pl.when(i == lo2)
            def _():
                save_x(prev).wait()
                save_u(prev).wait()

            @pl.when(jnp.logical_and(i >= lo2, i < lo2 + pieces))
            def _():
                second_product(prev, i - lo2, buf_b, s)

            @pl.when(i == 2 * NT + pieces - 1)
            def _():
                give_credits()
                normalize(1, True)

            @pl.when(i == 4 * NT + pieces - 1)
            def _():
                normalize(2, False)
            return carry

        lax.fori_loop(0, FUSED_FROM + LEAD, iteration, 0)

    pl.run_scoped(
        forward,
        pltpu.VMEM((2, HIDDEN, UP_TILE), BF16), pltpu.VMEM((2, FF, OUT_COLS), BF16),
        pltpu.VMEM((TOKENS, FF), BF16), pltpu.VMEM((2, TOKENS, UP_TILE), BF16),
    )

    loads[3].wait()

    last = LAYERS - 1

    def fused_loads(t, buf_a, buf_b):
        return (first_load(last, t, buf_a),
                pltpu.make_async_copy(land_down.at[last % 2, pl.ds(pl.multiple_of(UP_TILE * t, 16), UP_TILE), :], buf_b.at[lax.rem(t, 2)], w_sem.at[1, lax.rem(t, 2)]))

    def fused(buf_a, buf_b, dpre, y, acc, out):
        y[...] = jnp.zeros_like(y)
        acc[...] = jnp.zeros_like(acc)
        dlow[...] = jnp.zeros_like(dlow)
        for matrix in range(2):
            swap_own(LAYERS - 2, matrix).start()

        def iteration(i, carry):
            gather_step(i)
            n = i - FUSED_FROM
            send_back(n)

            @pl.when(n < NT)
            def _():
                for load in fused_loads(n, buf_a, buf_b):
                    load.start()

            @pl.when(n >= 1)
            def _():
                t = n - 1
                slot = lax.rem(t, 2)
                for load in fused_loads(t, buf_a, buf_b):
                    load.wait()
                c = pl.multiple_of(UP_TILE * t, LANES)

                for h in range(TOKENS // ROWS):
                    r = slice(ROWS * h, ROWS * h + ROWS)
                    pre = dot(u[r, :], buf_a[slot]) + dot(v6[r, :], b6[:, pl.ds(c, UP_TILE)])
                    dh = dot_t(d[r, :], buf_b[slot]).astype(BF16).astype(F32)
                    s, slope = gelu_both(pre.astype(BF16))
                    dp = (dh * slope).astype(BF16)
                    dpre[r, :] = dp
                    y[r, :] += dot(s.astype(BF16), buf_b[slot])
                    acc[r, :] += dot_t(dp, buf_a[slot])

                low_parts(last, dpre[...], c)
            return carry

        lax.fori_loop(FUSED_FROM, TILES + 1, iteration, 0)

        pl.loop(TILES + 1 - FUSED_FROM, 4 * SUBS)(send_back)

        @pl.loop(0, TOKENS // LANES)
        def _(i):
            r = pl.ds(pl.multiple_of(i * LANES, LANES), LANES)
            out[r, :] = (x[r, :].astype(F32) + y[r, :]).astype(BF16)

        out_copy = pltpu.make_async_copy(out, out_tokens, load_sem.at[6])
        out_copy.start()
        close_layer(last, acc)
        out_copy.wait()

    pl.run_scoped(
        fused,
        pltpu.VMEM((2, HIDDEN, UP_TILE), BF16), pltpu.VMEM((2, UP_TILE, HIDDEN), BF16), pltpu.VMEM((TOKENS, UP_TILE), BF16),
        pltpu.VMEM((TOKENS, HIDDEN), F32), pltpu.VMEM((TOKENS, HIDDEN), F32), pltpu.VMEM((TOKENS, HIDDEN), BF16),
    )

    steps = 2 * SUBS

    def backward(buf_a, buf_b, act, dpre, acc):
        def place(n):
            layer, b = (LAYERS - 2) - n // steps, lax.rem(n, steps)
            outside, sub = b // SUBS, lax.rem(b, SUBS)
            base = 2 * (parity + outside - 2 * parity * outside)
            return layer, b, outside, sub, [pl.multiple_of(QUARTER * (base + c) + SUB * sub, SUB) for c in (core, 1 - core)]

        def loads_of(n):
            layer, _, outside, sub, fs = place(n)
            s = lax.rem(n, 2)
            copies = []
            for i in range(2):
                half = pl.ds(SUB * i, SUB)
                copies += [(back_ref(0, layer, 2 * outside + i, sub), buf_a.at[s, :, half]), (back_ref(1, layer, 2 * outside + i, sub), buf_b.at[s, half, :]),
                           (pre_acts.at[layer, :, pl.ds(fs[i], SUB)], act.at[s, :, half])]
            return [pltpu.make_async_copy(src, dst, back_sem.at[s, i]) for i, (src, dst) in enumerate(copies)]

        def pass_on(n):
            layer, _, outside, sub, _ = place(n)

            @pl.when(jnp.logical_and(n < 2 * steps, outside == 1))
            def _():
                for matrix in range(2):
                    for axis in range(3):
                        back_copy(matrix, layer, sub, axis).wait_recv()
                    swap_sub(matrix, layer, sub).start()

        def fetch(n):
            layer, b, outside, sub, _ = place(n)

            @pl.when(b == 0)
            def _():
                for matrix in range(2):
                    swap_own(layer, matrix).wait_recv()

            @pl.when(outside == 1)
            def _():
                for matrix in range(2):
                    swap_sub(matrix, layer, sub).wait_recv()

            for load in loads_of(n):
                load.start()

        def reloads(layer):
            return (pltpu.make_async_copy(resids.at[layer], x, load_sem.at[4]), pltpu.make_async_copy(normeds.at[layer], u, load_sem.at[5]))

        for matrix in range(2):
            swap_own(0, matrix).start()
        fetch(0)

        def iteration(n, carry):
            layer, b, _, _, fs = place(n)
            s = lax.rem(n, 2)

            @pl.when(b == 0)
            def _():
                for load in reloads(layer):
                    load.start()
                adapters(layer)
                acc[...] = jnp.zeros_like(acc)
                dlow[...] = jnp.zeros_like(dlow)

            for stage in range(1, G_STAGES + 1):
                @pl.when(n == steps + 2 + stage)
                def _():
                    for done in range(1, LAYERS):
                        g_step(done, stage)
            for load in loads_of(n):
                load.wait()
            pass_on(n + 2)
            pl.when(n + 1 < 2 * steps)(lambda: fetch(n + 1))
            for h in range(TOKENS // ROWS):
                r = slice(ROWS * h, ROWS * h + ROWS)
                dh = dot_t(d[r, :], buf_b[s]).astype(BF16).astype(F32)
                _, slope = gelu_both(act[s, r, :])
                dp = (dh * slope).astype(BF16)
                dpre[r, :] = dp
                acc[r, :] += dot_t(dp, buf_a[s])
            for i in range(2):
                low_parts(layer, dpre[:, SUB * i:SUB * i + SUB], fs[i])

            @pl.when(b == steps - 1)
            def _():
                for load in reloads(layer):
                    load.wait()
                close_layer(layer, acc)
            return carry

        lax.fori_loop(0, 2 * steps, iteration, 0)
        grad_copy = pltpu.make_async_copy(d, grad_tokens, load_sem.at[6])
        grad_copy.start()
        for stage in range(1, G_STAGES + 1):
            g_step(0, stage)
        pl.loop(0, LAYERS)(g_finish)
        grad_copy.wait()

    pl.run_scoped(
        backward,
        pltpu.VMEM((2, HIDDEN, 2 * SUB), BF16), pltpu.VMEM((2, 2 * SUB, HIDDEN), BF16), pltpu.VMEM((2, TOKENS, 2 * SUB), BF16),
        pltpu.VMEM((TOKENS, 2 * SUB), BF16), pltpu.VMEM((TOKENS, HIDDEN), F32),
    )

    @pl.loop(0, LAYERS - 1)
    def _(layer):
        for matrix in range(2):
            swap_own(layer, matrix).wait_send()

            @pl.loop(0, SUBS)
            def _(sub):
                swap_sub(matrix, layer, sub).wait_send()
                for axis in range(3):
                    back_copy(matrix, layer, sub, axis).wait_send()


def step(tokens, cotangent, w_up, w_down, adapt_a, adapt_b):
    any_spec, vmem = pl.BlockSpec(memory_space=pl.ANY), pl.BlockSpec(memory_space=pltpu.VMEM)
    sds = jax.ShapeDtypeStruct
    dma = pltpu.SemaphoreType.DMA
    outs = [
        (sds((TOKENS, HIDDEN), BF16), any_spec), (sds((TOKENS, HIDDEN), BF16), any_spec),
        (sds((LAYERS, RANK, HIDDEN), F32), vmem), (sds((LAYERS, RANK, FF), F32), vmem),
        (sds((2, HIDDEN, FF), BF16), any_spec), (sds((2, FF, HIDDEN), BF16), any_spec),
        (sds((2, 4, HIDDEN, QUARTER), BF16), any_spec), (sds((2, 4, QUARTER, HIDDEN), BF16), any_spec),
        (sds((2, TOKENS, FF), BF16), any_spec), (sds((2, TOKENS, HIDDEN), BF16), any_spec), (sds((2, TOKENS, HIDDEN), BF16), any_spec),
    ]
    result = pl.pallas_call(
        step_kernel,
        out_shape=[o[0] for o in outs],
        in_specs=[any_spec] * 4 + [vmem] * 2,
        out_specs=[o[1] for o in outs],
        scratch_shapes=[
            pltpu.VMEM((LAYERS, UP_ROWS, FF), BF16), pltpu.VMEM((LAYERS, DOWN_ROWS, HIDDEN), BF16),
            pltpu.VMEM((TOKENS, HIDDEN), BF16), pltpu.VMEM((TOKENS, HIDDEN), BF16), pltpu.VMEM((TOKENS, HIDDEN), BF16),
            pltpu.VMEM((LAYERS, TOKENS, LANES), F32), pltpu.VMEM((LANES, FF), BF16), pltpu.VMEM((LANES, HIDDEN), BF16),
            pltpu.VMEM((TOKENS, LANES), BF16), pltpu.VMEM((LAYERS, 24, TOKENS), F32), pltpu.VMEM((8, TOKENS), F32), pltpu.VMEM((8, FF), F32),
            pltpu.VMEM((LAYERS, 8, G_COLS), F32), pltpu.VMEM((LAYERS, 5, 8, G_HALF), F32), pltpu.VMEM((LAYERS, 8, G_HALF), F32),
            pltpu.VMEM((LAYERS, 4, 8, G_HALF), F32), pltpu.VMEM((LAYERS, 8, G_HALF), F32),
            dma((RING, 16)), dma((RING, 4)), dma((SRING, 22)), dma((2, 2, SUBS, 3)), dma((2, 2, SUBS, 3)), dma((2, 2, SUBS + 1)), dma((2, 2, SUBS + 1)),
            dma((LAYERS, G_STAGES)), dma((LAYERS, G_STAGES)), dma((7,)), dma((2, 6)), dma((2, 2)), dma((2,)), dma((3,)), pltpu.SemaphoreType.REGULAR,
        ],
        compiler_params=pltpu.CompilerParams(collective_id=0, has_side_effects=True, vmem_limit_bytes=67_000_000),
        cost_estimate=pl.CostEstimate(flops=12 * 2 * TOKENS * HIDDEN * FF, bytes_accessed=400_000_000, transcendentals=0),
        name="mlp_stack",
    )(tokens, cotangent, w_up, w_down, jnp.swapaxes(adapt_a, 1, 2), adapt_b)
    return result[0], result[1], jnp.swapaxes(result[2], 1, 2), result[3]


def solution(mesh):
    tok_spec, weight_spec = P(GROUP, None), P(None, GROUP, None)
    return jax.shard_map(step, mesh=mesh, in_specs=(tok_spec, tok_spec, weight_spec, weight_spec, P(), P()), out_specs=(tok_spec, tok_spec, P(), P()), check_vma=False)
```

time: 2180 us -> 465 us (0.21)
  waiting for transfers between devices: 1640 us -> 0 us
  Pallas kernels: 0 us -> 458 us
  matrix products: 445 us -> 0 us
  blocking collectives: 39.3 us -> 0 us
    all_gather x12 -> x0, waiting for transfers between devices: 1500 us -> none  [the longest x3 533 us: device_step(): full_up = lax.all_gather(keep_up, 'local', axis=0, tiled=True)]
    pallas_call x0 -> x1, Pallas kernels: none -> 458 us  [step(): pl.pallas_call(step_kernel, out_shape=[o[0] for o in outs], in_specs=[any...]
    dot_general x30 -> x0, matrix products: 445 us -> none  [the longest x3 96.2 us: layer_backward(): jnp.einsum('th,fh->tf', d_resid, full_down, preferred_element_type=jnp.fl...]
    psum x1 -> x0, waiting for transfers between devices: 128 us -> none  [device_step(): grad_a, grad_b = lax.psum((grad_a, grad_b), GROUP)]
    psum x1 -> x0, blocking collectives: 39.3 us -> none  [device_step(): grad_a, grad_b = lax.psum((grad_a, grad_b), GROUP)]
    dynamic_slice x6 -> x0, local copies, waits for them, and re-layouts: 23 us -> none  [the longest x3 11.7 us: device_step(): lax.dynamic_slice_in_dim(full_up, local_idx * up_rows, up_rows, axis=0)]
  transfers between devices with their start and end apart: 13 -> 0, of which waited for: 13 -> 0; matrix products, arithmetic and copies ran while one was open for 21% -> 0% of each run, Pallas kernels for 0% -> 0%
where the time goes in v1:
time: 465 us
  Pallas kernels  458 us (98%)
  local copies, waits for them, and re-layouts  6.37 us (1%)
    pallas_call x1, Pallas kernels, step(): pl.pallas_call(step_kernel, out_shape=[o[0] for o in outs], in_specs=[any...  458 us

profile of v1, /device:TPU:0, one launch (start us, length us, event | category | flops | bytes accessed | tf_op | source)
XLA Modules:
  0.0 465.3 jit_solution(14590423891641345995)
XLA Ops:
  0.6 458.2 %mlp_stack.1 = (bf16[1024,1280]{1,0:T(8,128)(2,1)}, bf16[1024,1280]{1,0:T(8,128)(2,1)}, f32[3,4,1280]{2,1,0:T(4,128)}, f32[3,4,5120]{2,1,0:T(4,128)}, bf16[2,128...) custom-call(bf16[1024,1280]{1,0:T(8,128)(2,1)} %tokens.1, ...), custom_call_target="tpu_custom_call" | custom-call | flops 161061273600 | bytes 400000000 | tf_op jit(solution)/shard_map/mlp_stack/pallas_call | solution.py:711
  458.9 0.0 copy-start
  458.9 3.6 copy.14
  462.4 0.0 copy-done
  462.4 0.0 copy-start.2
  462.4 0.0 copy-start.1
  462.4 1.5 copy.15
  463.9 0.0 copy-done.2
  463.9 0.6 copy.16
  464.6 0.0 copy-done.1
  464.6 0.7 copy.17
Async XLA Ops:
  458.9 3.6 copy-start
  462.4 1.5 copy-start.2
  462.4 2.1 copy-start.1

commit v2 on v1

--- a/solution.py
+++ b/solution.py
@@ -23,10 +23,19 @@
 UP_TILE, DOWN_TILE = FF // NT, DOWN_ROWS // NT
 OUT_COLS = 256
 QUARTER = FF // 4
-RING, SRING = 20, 16
+RING, SRING = 28, 16
 OFFSETS = (7, 6, 5, 4, 3, 2, 1, 0, -1)
 LEAD = OFFSETS[0]
-FUSED_FROM = 5 * NT
+FAR_LEAD = 2 * LEAD - 1
+MIX = 4 * NT
+FUSED_FROM = MIX + HIDDEN // OUT_COLS
+FUSED_TO = FUSED_FROM + 2 * NT - 2
+BACK_FROM = 48
+BACK_EARLY, BACK_EVERY = 3, 3
+BACK_STEADY = BACK_FROM + BACK_EVERY * BACK_EARLY - 1
+BACK_SENT = BACK_EARLY + FUSED_TO - BACK_STEADY
+BACK_AHEAD = 2
+SUMS_FROM = 14
 SUB = 256
 SUBS = QUARTER // SUB
 G_COLS = 3328
@@ -73,8 +82,8 @@
 def step_kernel(
     tokens, cotangent, w_up, w_down, adapt_a, adapt_b,
     out_tokens, grad_tokens, grad_a, grad_b,
-    land_up, land_down, back_up, back_down, pre_acts, resids, normeds,
-    own_up, own_down, x, u, d, inv_s, b6, a6, v6, v3, dlow, gb, send_g, half_g, recv_first, recv_half, recv_last,
+    land_up, land_down, back_up, back_down, slopes, resids, normeds,
+    own_up, own_down, x, u, d, inv_s, b6, a6, v6, v3, perm, dlow, gb, send_g, half_g, recv_first, recv_half, recv_last,
     recv_sem, pair_sem, send_sem, back_recv, back_send, swap_recv, swap_send, g_recv, g_send, load_sem, back_sem, w_sem, act_sem, keep_sem, credit,
 ):
     z = lax.axis_index("local")
@@ -126,11 +135,13 @@
     loads[1].wait()
 
     def is_up(k):
-        m = k // NT
-        return jnp.logical_or(jnp.logical_and(lax.rem(m, 2) == 0, m < 4), m == 5)
+        return jnp.where(k < MIX, lax.rem(k // NT, 2) == 0, lax.rem(k, 2) == 1)
+
+    def tile_of(k):
+        return jnp.where(k < MIX, lax.rem(k, NT), (k - MIX) // 2)
 
     def slab(up, k, col, zz, own=False):
-        layer, t, n = k // (2 * NT), lax.rem(k, NT), 4 * col + zz
+        layer, t, n = k // (2 * NT), tile_of(k), 4 * col + zz
         slot = lax.rem(layer, 2)
         if up:
             c = pl.ds(pl.multiple_of(UP_TILE * t, LANES), UP_TILE)
@@ -150,7 +161,7 @@
         remote(s, s, send_sem.at[0, 0], recv_sem.at[lax.rem(k, RING), rel * 4 + zz], to_x).wait_recv()
 
     def pair_copy(up, k, g, c):
-        layer, t = k // (2 * NT), lax.rem(k, NT)
+        layer, t = k // (2 * NT), tile_of(k)
         slot = lax.rem(layer, 2)
         if up:
             s = land_up.at[slot, pl.ds(pl.multiple_of(4 * UP_ROWS * c, 8), 4 * UP_ROWS), pl.ds(pl.multiple_of(UP_TILE * t, LANES), UP_TILE)]
@@ -240,15 +251,21 @@
         for g in range(4):
             pair_copy(up, k, g, cols[g]).wait_send()
 
-    stages = list(zip(OFFSETS[::-1], (stage_sent, stage_done, stage_pair, stage_swap, stage_diag, stage_3, stage_2, stage_1, stage_own)))
+    stages = list(zip(OFFSETS[:0:-1], (stage_sent, stage_done, stage_pair, stage_swap, stage_diag, stage_3, stage_2, stage_1)))
+
+    def at_tile(k, stage):
+        @pl.when(jnp.logical_and(k >= 0, k < TILES))
+        def _():
+            both(is_up(k), lambda: stage(True, k), lambda: stage(False, k))
 
     def gather_step(i):
         for offset, stage in stages:
-            k = i + offset
-
-            @pl.when(jnp.logical_and(k >= 0, k < TILES))
-            def _():
-                both(is_up(k), lambda: stage(True, k), lambda: stage(False, k))
+            at_tile(i + offset, stage)
+        first = jnp.minimum(2 * (i + LEAD), i + FAR_LEAD)
+
+        @pl.loop(first, jnp.minimum(2 * (i + LEAD) + 2, i + FAR_LEAD + 1))
+        def _(k):
+            at_tile(k, stage_own)
 
     def give_credits():
         for target in (to_p, to_x, to_y, to_c):
@@ -332,9 +349,34 @@
     def rows8(value):
         return jnp.concatenate([value, jnp.zeros_like(value)], axis=0)
 
-    def adapters(layer):
+    def build_order():
+        @pl.loop(0, HIDDEN // OUT_COLS)
+        def _(block):
+            o = lax.broadcasted_iota(jnp.int32, (HIDDEN, OUT_COLS), 1) + OUT_COLS * block
+            c = lax.broadcasted_iota(jnp.int32, (HIDDEN, OUT_COLS), 0)
+            tile, place = o // LANES, o % LANES
+            source = DOWN_ROWS * (place // DOWN_TILE) + DOWN_TILE * tile + place % DOWN_TILE
+            perm[:, pl.ds(pl.multiple_of(OUT_COLS * block, OUT_COLS), OUT_COLS)] = jnp.where(c == source, 1.0, 0.0).astype(BF16)
+
+        parts = FF // HIDDEN
+        moved = [dot(own_up[LAYERS - 1, :, HIDDEN * m:HIDDEN * m + HIDDEN], perm[...]).astype(BF16) for m in range(parts)]
+        for m in range(parts):
+            for tile in range(NT):
+                first = UP_TILE * tile + LANES * m
+                own_up[LAYERS - 1, :, first:first + LANES] = moved[m][:, LANES * tile:LANES * tile + LANES]
+
+    def adapters(layer, reorder=False):
         for c in range(0, FF, HIDDEN):
-            write_blocks(b6.at[:, c:c + HIDDEN], stack_right(rows8(adapt_b[layer, :, c:c + HIDDEN])))
+            blocks = stack_right(rows8(adapt_b[layer, :, c:c + HIDDEN]))
+            if reorder:
+                moved = dot(jnp.concatenate([*blocks[:3], blocks[0]], axis=0).astype(BF16), perm[...])
+                for tile in range(NT):
+                    o = slice(LANES * tile, LANES * tile + LANES)
+                    hi, mid, lo = moved[0:8, o], moved[8:16, o], moved[16:24, o]
+                    first = UP_TILE * tile + c // HIDDEN * LANES
+                    write_blocks(b6.at[:, first:first + LANES], (hi, mid, lo, hi, mid, hi))
+            else:
+                write_blocks(b6.at[:, c:c + HIDDEN], blocks)
         write_blocks(a6, stack_right(rows8(adapt_a[layer])))
 
     def normalize(layer, save):
@@ -346,7 +388,8 @@
             u[r, :] = (xf * inv).astype(BF16)
             inv_s[layer, r, :] = jnp.broadcast_to(inv, (LANES, LANES))
 
-        adapters(layer)
+        if layer < LAYERS - 1:
+            adapters(layer)
         low = sum3(dot_t(a6[0:32, :], u[...]))
         left = stack_left(low)
         v3[layer, :, :] = jnp.concatenate([left[0], left[3], left[5]], axis=0)
@@ -366,7 +409,7 @@
         return pltpu.make_async_copy(land_up.at[lax.rem(layer, 2), :, pl.ds(pl.multiple_of(UP_TILE * t, LANES), UP_TILE)], buf.at[lax.rem(t, 2)], w_sem.at[0, lax.rem(t, 2)])
 
     def act_store(layer, t, acts):
-        return pltpu.make_async_copy(acts.at[lax.rem(t, 2)], pre_acts.at[layer, :, pl.ds(pl.multiple_of(UP_TILE * t, LANES), UP_TILE)], act_sem.at[lax.rem(t, 2)])
+        return pltpu.make_async_copy(acts.at[lax.rem(t, 2)], slopes.at[layer, :, pl.ds(pl.multiple_of(UP_TILE * t, LANES), UP_TILE)], act_sem.at[lax.rem(t, 2)])
 
     def keep_half(layer, t, h, buf):
         block = 2 * t + h - 5 * quarter
@@ -387,11 +430,9 @@
         c = pl.ds(pl.multiple_of(UP_TILE * t, LANES), UP_TILE)
         pre = dot(u[...], buf[lax.rem(t, 2)]) + dot(v6[...], b6[:, c])
         act = pre.astype(BF16)
-        acts[lax.rem(t, 2)] = act
-        af = act.astype(F32)
-        _, th = gelu_inner(af)
-        half = 0.5 * af
-        s[:, c] = (half + half * th).astype(BF16)
+        hidden, slope = gelu_both(act)
+        s[:, c] = hidden.astype(BF16)
+        acts[lax.rem(t, 2)] = slope
         act_store(layer, t, acts).start()
         for h in range(2):
             cond, copy = keep_half(layer, t, h, buf)
@@ -419,10 +460,19 @@
         slope = 0.5 + 0.5 * th + half * (1.0 - th * th) * (GELU_S + (3.0 * GELU_S * GELU_C) * x2)
         return half + half * th, slope
 
-    def low_parts(layer, dpre, c):
-        cc = pl.ds(c, dpre.shape[1])
-        dlow[...] += sum3(dot_t(b6[0:32, cc], dpre))
-        gb[:, cc] = sum3(dot(v3[layer].astype(BF16), dpre))
+    def low_parts(layer, dpre, *places):
+        width = dpre.shape[1] // len(places)
+        dlow[...] += sum3(dot_t(jnp.concatenate([b6[0:32, pl.ds(c, width)] for c in places], axis=1), dpre))
+        share = sum3(dot(v3[layer].astype(BF16), dpre))
+        for i, c in enumerate(places):
+            gb[:, pl.ds(c, width)] = share[:, width * i:width * i + width]
+
+    def natural_order():
+        for m in range(FF // HIDDEN):
+            piece = jnp.concatenate([grad_b[LAYERS - 1, :, UP_TILE * tile + LANES * m:UP_TILE * tile + LANES * m + LANES] for tile in range(NT)], axis=1)
+            parts = jnp.concatenate(split3(rows8(piece)), axis=0).astype(BF16)
+            gb[:, HIDDEN * m:HIDDEN * m + HIDDEN] = sum3(dot_t(parts, perm[...]))
+        grad_b[LAYERS - 1, :, :] = gb[0:RANK, :]
 
     def close_layer(layer, acc):
         left = stack_left(dlow[...])
@@ -436,9 +486,10 @@
         send_g[layer, :, G_EDGE:G_COLS] = jnp.zeros((8, G_COLS - G_EDGE), F32)
         g_step(layer, 0)
 
-        @pl.loop(0, TOKENS // LANES)
+        @pl.loop(0, TOKENS // OUT_COLS)
         def _(i):
-            r = pl.ds(pl.multiple_of(i * LANES, LANES), LANES)
+            r = pl.ds(pl.multiple_of(i * OUT_COLS, OUT_COLS), OUT_COLS)
+            pl.when(jnp.logical_and(layer == 0, i == 1))(lambda: g_step(0, 1))
             side = dot(v6[r, :], a6[...]).astype(BF16)
             dn = (acc[r, :].astype(BF16) + side).astype(F32)
             xf = x[r, :].astype(F32)
@@ -455,7 +506,7 @@
         def iteration(j, carry):
             i = j - LEAD
 
-            pl.when(i == 2 * 2 * NT - LEAD)(wait_credits)
+            pl.when(i == MIX - FAR_LEAD)(wait_credits)
             gather_step(i)
 
             @pl.when(i == -2)
@@ -480,6 +531,8 @@
                 act_store(layer, NT - 2, acts).wait()
                 act_store(layer, NT - 1, acts).wait()
 
+            pl.when(i == NT + 2)(build_order)
+            pl.when(i == MIX - 3)(lambda: adapters(LAYERS - 1, reorder=True))
             pieces = HIDDEN // OUT_COLS
             prev = jnp.where(i >= 4 * NT - 1, 1, 0)
             lo2 = 2 * NT + 2 * NT * prev
@@ -512,7 +565,7 @@
     pl.run_scoped(
         forward,
         pltpu.VMEM((2, HIDDEN, UP_TILE), BF16), pltpu.VMEM((2, FF, OUT_COLS), BF16),
-        pltpu.VMEM((TOKENS, FF), BF16), pltpu.VMEM((2, TOKENS, UP_TILE), BF16),
+        pltpu.VMEM((TOKENS, FF), BF16), pltpu.VMEM((2, TOKENS, UP_TILE), F32),
     )
 
     loads[3].wait()
@@ -520,8 +573,8 @@
     last = LAYERS - 1
 
     def fused_loads(t, buf_a, buf_b):
-        return (first_load(last, t, buf_a),
-                pltpu.make_async_copy(land_down.at[last % 2, pl.ds(pl.multiple_of(UP_TILE * t, 16), UP_TILE), :], buf_b.at[lax.rem(t, 2)], w_sem.at[1, lax.rem(t, 2)]))
+        rows = land_down.reshape(2, 32, DOWN_ROWS, HIDDEN).at[last % 2, :, pl.ds(pl.multiple_of(DOWN_TILE * t, 16), DOWN_TILE), :]
+        return first_load(last, t, buf_a), pltpu.make_async_copy(rows, buf_b.at[lax.rem(t, 2)], w_sem.at[1, lax.rem(t, 2)])
 
     def fused(buf_a, buf_b, dpre, y, acc, out):
         y[...] = jnp.zeros_like(y)
@@ -530,40 +583,54 @@
         for matrix in range(2):
             swap_own(LAYERS - 2, matrix).start()
 
+        for load in fused_loads(0, buf_a, buf_b):
+            load.start()
+
         def iteration(i, carry):
             gather_step(i)
-            n = i - FUSED_FROM
-            send_back(n)
-
-            @pl.when(n < NT)
-            def _():
-                for load in fused_loads(n, buf_a, buf_b):
+            early, ticks = i - BACK_FROM, lax.rem(i - BACK_FROM, BACK_EVERY)
+            pl.when(jnp.logical_and(jnp.logical_and(early >= 0, i < BACK_STEADY), ticks == 0))(lambda: send_back(early // BACK_EVERY))
+            pl.when(i >= BACK_STEADY)(lambda: send_back(BACK_EARLY + i - BACK_STEADY))
+
+            catch_up = i < FUSED_FROM + 2
+            t_load = jnp.where(i == FUSED_FROM, 1, (i - MIX - 2) // 2)
+
+            @pl.when(jnp.logical_and(jnp.logical_or(i == FUSED_FROM, lax.rem(i, 2) == 0), t_load < NT))
+            def _():
+                for load in fused_loads(t_load, buf_a, buf_b):
                     load.start()
 
-            @pl.when(n >= 1)
-            def _():
-                t = n - 1
+            first_half = jnp.where(catch_up, 2 * (i - FUSED_FROM), i - FUSED_FROM + 2)
+
+            @pl.loop(first_half, jnp.where(catch_up, first_half + 2, first_half + 1))
+            def _(g):
+                t, h = g // 2, lax.rem(g, 2)
                 slot = lax.rem(t, 2)
-                for load in fused_loads(t, buf_a, buf_b):
-                    load.wait()
+
+                @pl.when(h == 0)
+                def _():
+                    for load in fused_loads(t, buf_a, buf_b):
+                        load.wait()
+
                 c = pl.multiple_of(UP_TILE * t, LANES)
-
-                for h in range(TOKENS // ROWS):
-                    r = slice(ROWS * h, ROWS * h + ROWS)
-                    pre = dot(u[r, :], buf_a[slot]) + dot(v6[r, :], b6[:, pl.ds(c, UP_TILE)])
-                    dh = dot_t(d[r, :], buf_b[slot]).astype(BF16).astype(F32)
-                    s, slope = gelu_both(pre.astype(BF16))
-                    dp = (dh * slope).astype(BF16)
-                    dpre[r, :] = dp
-                    y[r, :] += dot(s.astype(BF16), buf_b[slot])
-                    acc[r, :] += dot_t(dp, buf_a[slot])
-
-                low_parts(last, dpre[...], c)
+                r = pl.ds(pl.multiple_of(ROWS * h, ROWS), ROWS)
+                down = buf_b.at[slot]
+                pre = dot(u[r, :], buf_a[slot]) + dot(v6[r, :], b6[:, pl.ds(c, UP_TILE)])
+                dh = dot_t(d[r, :], down[...].reshape(UP_TILE, HIDDEN)).astype(BF16).astype(F32)
+                s, slope = gelu_both(pre.astype(BF16))
+                dp = (dh * slope).astype(BF16)
+                dpre[r, :] = dp
+                y[r, :] += dot(s.astype(BF16), down[...].reshape(UP_TILE, HIDDEN))
+                acc[r, :] += dot_t(dp, buf_a[slot])
+
+                @pl.when(h == 1)
+                def _():
+                    low_parts(last, dpre[...], c)
             return carry
 
-        lax.fori_loop(FUSED_FROM, TILES + 1, iteration, 0)
-
-        pl.loop(TILES + 1 - FUSED_FROM, 4 * SUBS)(send_back)
+        lax.fori_loop(FUSED_FROM, FUSED_TO, iteration, 0)
+
+        pl.loop(BACK_SENT, BACK_SENT + BACK_AHEAD)(send_back)
 
         @pl.loop(0, TOKENS // LANES)
         def _(i):
@@ -577,7 +644,7 @@
 
     pl.run_scoped(
         fused,
-        pltpu.VMEM((2, HIDDEN, UP_TILE), BF16), pltpu.VMEM((2, UP_TILE, HIDDEN), BF16), pltpu.VMEM((TOKENS, UP_TILE), BF16),
+        pltpu.VMEM((2, HIDDEN, UP_TILE), BF16), pltpu.VMEM((2, 32, DOWN_TILE, HIDDEN), BF16), pltpu.VMEM((TOKENS, UP_TILE), BF16),
         pltpu.VMEM((TOKENS, HIDDEN), F32), pltpu.VMEM((TOKENS, HIDDEN), F32), pltpu.VMEM((TOKENS, HIDDEN), BF16),
     )
 
@@ -597,7 +664,7 @@
             for i in range(2):
                 half = pl.ds(SUB * i, SUB)
                 copies += [(back_ref(0, layer, 2 * outside + i, sub), buf_a.at[s, :, half]), (back_ref(1, layer, 2 * outside + i, sub), buf_b.at[s, half, :]),
-                           (pre_acts.at[layer, :, pl.ds(fs[i], SUB)], act.at[s, :, half])]
+                           (slopes.at[layer, :, pl.ds(fs[i], SUB)], act.at[s, :, half])]
             return [pltpu.make_async_copy(src, dst, back_sem.at[s, i]) for i, (src, dst) in enumerate(copies)]
 
         def pass_on(n):
@@ -645,11 +712,11 @@
                 acc[...] = jnp.zeros_like(acc)
                 dlow[...] = jnp.zeros_like(dlow)
 
+            h = n + BACK_SENT + BACK_AHEAD
+            pl.when(h < 4 * SUBS)(lambda: send_back(h))
             for stage in range(1, G_STAGES + 1):
-                @pl.when(n == steps + 2 + stage)
-                def _():
-                    for done in range(1, LAYERS):
-                        g_step(done, stage)
+                for done in range(1, LAYERS):
+                    pl.when(n == SUMS_FROM + stage - done)(lambda: g_step(done, stage))
             for load in loads_of(n):
                 load.wait()
             pass_on(n + 2)
@@ -657,12 +724,10 @@
             for h in range(TOKENS // ROWS):
                 r = slice(ROWS * h, ROWS * h + ROWS)
                 dh = dot_t(d[r, :], buf_b[s]).astype(BF16).astype(F32)
-                _, slope = gelu_both(act[s, r, :])
-                dp = (dh * slope).astype(BF16)
+                dp = (dh * act[s, r, :]).astype(BF16)
                 dpre[r, :] = dp
                 acc[r, :] += dot_t(dp, buf_a[s])
-            for i in range(2):
-                low_parts(layer, dpre[:, SUB * i:SUB * i + SUB], fs[i])
+            low_parts(layer, dpre[...], *fs)
 
             @pl.when(b == steps - 1)
             def _():
@@ -674,14 +739,17 @@
         lax.fori_loop(0, 2 * steps, iteration, 0)
         grad_copy = pltpu.make_async_copy(d, grad_tokens, load_sem.at[6])
         grad_copy.start()
-        for stage in range(1, G_STAGES + 1):
+        g_step(0, 2)
+        pl.loop(1, LAYERS)(g_finish)
+        natural_order()
+        for stage in range(3, G_STAGES + 1):
             g_step(0, stage)
-        pl.loop(0, LAYERS)(g_finish)
+        g_finish(0)
         grad_copy.wait()
 
     pl.run_scoped(
         backward,
-        pltpu.VMEM((2, HIDDEN, 2 * SUB), BF16), pltpu.VMEM((2, 2 * SUB, HIDDEN), BF16), pltpu.VMEM((2, TOKENS, 2 * SUB), BF16),
+        pltpu.VMEM((2, HIDDEN, 2 * SUB), BF16), pltpu.VMEM((2, 2 * SUB, HIDDEN), BF16), pltpu.VMEM((2, TOKENS, 2 * SUB), F32),
         pltpu.VMEM((TOKENS, 2 * SUB), BF16), pltpu.VMEM((TOKENS, HIDDEN), F32),
     )
 
@@ -706,7 +774,7 @@
         (sds((LAYERS, RANK, HIDDEN), F32), vmem), (sds((LAYERS, RANK, FF), F32), vmem),
         (sds((2, HIDDEN, FF), BF16), any_spec), (sds((2, FF, HIDDEN), BF16), any_spec),
         (sds((2, 4, HIDDEN, QUARTER), BF16), any_spec), (sds((2, 4, QUARTER, HIDDEN), BF16), any_spec),
-        (sds((2, TOKENS, FF), BF16), any_spec), (sds((2, TOKENS, HIDDEN), BF16), any_spec), (sds((2, TOKENS, HIDDEN), BF16), any_spec),
+        (sds((2, TOKENS, FF), F32), any_spec), (sds((2, TOKENS, HIDDEN), BF16), any_spec), (sds((2, TOKENS, HIDDEN), BF16), any_spec),
     ]
     result = pl.pallas_call(
         step_kernel,
@@ -717,7 +785,7 @@
             pltpu.VMEM((LAYERS, UP_ROWS, FF), BF16), pltpu.VMEM((LAYERS, DOWN_ROWS, HIDDEN), BF16),
             pltpu.VMEM((TOKENS, HIDDEN), BF16), pltpu.VMEM((TOKENS, HIDDEN), BF16), pltpu.VMEM((TOKENS, HIDDEN), BF16),
             pltpu.VMEM((LAYERS, TOKENS, LANES), F32), pltpu.VMEM((LANES, FF), BF16), pltpu.VMEM((LANES, HIDDEN), BF16),
-            pltpu.VMEM((TOKENS, LANES), BF16), pltpu.VMEM((LAYERS, 24, TOKENS), F32), pltpu.VMEM((8, TOKENS), F32), pltpu.VMEM((8, FF), F32),
+            pltpu.VMEM((TOKENS, LANES), BF16), pltpu.VMEM((LAYERS, 24, TOKENS), F32), pltpu.VMEM((HIDDEN, HIDDEN), BF16), pltpu.VMEM((8, TOKENS), F32), pltpu.VMEM((8, FF), F32),
             pltpu.VMEM((LAYERS, 8, G_COLS), F32), pltpu.VMEM((LAYERS, 5, 8, G_HALF), F32), pltpu.VMEM((LAYERS, 8, G_HALF), F32),
             pltpu.VMEM((LAYERS, 4, 8, G_HALF), F32), pltpu.VMEM((LAYERS, 8, G_HALF), F32),
             dma((RING, 16)), dma((RING, 4)), dma((SRING, 22)), dma((2, 2, SUBS, 3)), dma((2, 2, SUBS, 3)), dma((2, 2, SUBS + 1)), dma((2, 2, SUBS + 1)),

time: 465 us -> 447 us (0.961)
  Pallas kernels: 458 us -> 440 us
    pallas_call x1, Pallas kernels: 458 us -> 440 us  [step(): pl.pallas_call(step_kernel, out_shape=[o[0] for o in outs], in_specs=[any...]
where the time goes in v2:
time: 447 us
  Pallas kernels  440 us (98%)
  local copies, waits for them, and re-layouts  6.37 us (1%)
    pallas_call x1, Pallas kernels, step(): pl.pallas_call(step_kernel, out_shape=[o[0] for o in outs], in_specs=[any...  440 us

profile of v2, /device:TPU:0, one launch (start us, length us, event | category | flops | bytes accessed | tf_op | source)
XLA Modules:
  0.0 447.1 jit_solution(8095886423890402497)
XLA Ops:
  0.6 440.1 %mlp_stack.1 = (bf16[1024,1280]{1,0:T(8,128)(2,1)}, bf16[1024,1280]{1,0:T(8,128)(2,1)}, f32[3,4,1280]{2,1,0:T(4,128)}, f32[3,4,5120]{2,1,0:T(4,128)}, bf16[2,128...) custom-call(bf16[1024,1280]{1,0:T(8,128)(2,1)} %tokens.1, ...), custom_call_target="tpu_custom_call" | custom-call | flops 161061273600 | bytes 400000000 | tf_op jit(solution)/shard_map/mlp_stack/pallas_call | solution.py:779
  440.7 0.0 copy-start
  440.7 3.6 copy.14
  444.3 0.0 copy-done
  444.3 0.0 copy-start.2
  444.3 0.0 copy-start.1
  444.3 1.5 copy.15
  445.8 0.0 copy-done.2
  445.8 0.6 copy.16
  446.4 0.0 copy-done.1
  446.4 0.7 copy.17
Async XLA Ops:
  440.7 3.6 copy-start
  444.3 1.5 copy-start.2
  444.3 2.1 copy-start.1

commit v3 on v2

--- a/solution.py
+++ b/solution.py
@@ -359,7 +359,7 @@
             perm[:, pl.ds(pl.multiple_of(OUT_COLS * block, OUT_COLS), OUT_COLS)] = jnp.where(c == source, 1.0, 0.0).astype(BF16)
 
         parts = FF // HIDDEN
-        moved = [dot(own_up[LAYERS - 1, :, HIDDEN * m:HIDDEN * m + HIDDEN], perm[...]).astype(BF16) for m in range(parts)]
+        moved = [dot(own_up[LAYERS - 1, :, HIDDEN * m:HIDDEN * m + HIDDEN], perm[:]).astype(BF16) for m in range(parts)]
         for m in range(parts):
             for tile in range(NT):
                 first = UP_TILE * tile + LANES * m
@@ -369,7 +369,7 @@
         for c in range(0, FF, HIDDEN):
             blocks = stack_right(rows8(adapt_b[layer, :, c:c + HIDDEN]))
             if reorder:
-                moved = dot(jnp.concatenate([*blocks[:3], blocks[0]], axis=0).astype(BF16), perm[...])
+                moved = dot(jnp.concatenate([*blocks[:3], blocks[0]], axis=0).astype(BF16), perm[:])
                 for tile in range(NT):
                     o = slice(LANES * tile, LANES * tile + LANES)
                     hi, mid, lo = moved[0:8, o], moved[8:16, o], moved[16:24, o]
@@ -390,11 +390,11 @@
 
         if layer < LAYERS - 1:
             adapters(layer)
-        low = sum3(dot_t(a6[0:32, :], u[...]))
+        low = sum3(dot_t(a6[0:32, :], u[:]))
         left = stack_left(low)
         v3[layer, :, :] = jnp.concatenate([left[0], left[3], left[5]], axis=0)
         wide = jnp.concatenate(list(left) + [jnp.zeros((80, TOKENS), F32)], axis=0)
-        v6[...] = jnp.transpose(wide).astype(BF16)
+        v6[:] = jnp.transpose(wide).astype(BF16)
         if save:
             save_x(layer).start()
             save_u(layer).start()
@@ -428,7 +428,7 @@
             act_store(layer, t - 2, acts).wait()
 
         c = pl.ds(pl.multiple_of(UP_TILE * t, LANES), UP_TILE)
-        pre = dot(u[...], buf[lax.rem(t, 2)]) + dot(v6[...], b6[:, c])
+        pre = dot(u[:], buf[lax.rem(t, 2)]) + dot(v6[:], b6[:, c])
         act = pre.astype(BF16)
         hidden, slope = gelu_both(act)
         s[:, c] = hidden.astype(BF16)
@@ -450,7 +450,7 @@
         keep = second_keep(layer, c, buf)
         keep.start()
         cc = pl.ds(pl.multiple_of(OUT_COLS * c, LANES), OUT_COLS)
-        x[:, cc] = (x[:, cc].astype(F32) + dot(s[...], buf[lax.rem(c, 2)])).astype(BF16)
+        x[:, cc] = (x[:, cc].astype(F32) + dot(s[:], buf[lax.rem(c, 2)])).astype(BF16)
         keep.wait()
 
     def gelu_both(act):
@@ -462,7 +462,7 @@
 
     def low_parts(layer, dpre, *places):
         width = dpre.shape[1] // len(places)
-        dlow[...] += sum3(dot_t(jnp.concatenate([b6[0:32, pl.ds(c, width)] for c in places], axis=1), dpre))
+        dlow[:] += sum3(dot_t(jnp.concatenate([b6[0:32, pl.ds(c, width)] for c in places], axis=1), dpre))
         share = sum3(dot(v3[layer].astype(BF16), dpre))
         for i, c in enumerate(places):
             gb[:, pl.ds(c, width)] = share[:, width * i:width * i + width]
@@ -471,15 +471,15 @@
         for m in range(FF // HIDDEN):
             piece = jnp.concatenate([grad_b[LAYERS - 1, :, UP_TILE * tile + LANES * m:UP_TILE * tile + LANES * m + LANES] for tile in range(NT)], axis=1)
             parts = jnp.concatenate(split3(rows8(piece)), axis=0).astype(BF16)
-            gb[:, HIDDEN * m:HIDDEN * m + HIDDEN] = sum3(dot_t(parts, perm[...]))
+            gb[:, HIDDEN * m:HIDDEN * m + HIDDEN] = sum3(dot_t(parts, perm[:]))
         grad_b[LAYERS - 1, :, :] = gb[0:RANK, :]
 
     def close_layer(layer, acc):
-        left = stack_left(dlow[...])
+        left = stack_left(dlow[:])
         wide = jnp.concatenate(list(left) + [jnp.zeros((80, TOKENS), F32)], axis=0)
-        v6[...] = jnp.transpose(wide).astype(BF16)
+        v6[:] = jnp.transpose(wide).astype(BF16)
         narrow = jnp.concatenate([left[0], left[3], left[5]], axis=0).astype(BF16)
-        ga = sum3(dot(narrow, u[...]))
+        ga = sum3(dot(narrow, u[:]))
         send_g[layer, 0:RANK, 0:G_EDGE] = gb[0:RANK, 0:G_EDGE]
         send_g[layer, RANK:2 * RANK, 0:FF - G_EDGE] = gb[0:RANK, G_EDGE:FF]
         send_g[layer, RANK:2 * RANK, FF - G_EDGE:G_EDGE] = ga[0:RANK]
@@ -490,7 +490,7 @@
         def _(i):
             r = pl.ds(pl.multiple_of(i * OUT_COLS, OUT_COLS), OUT_COLS)
             pl.when(jnp.logical_and(layer == 0, i == 1))(lambda: g_step(0, 1))
-            side = dot(v6[r, :], a6[...]).astype(BF16)
+            side = dot(v6[r, :], a6[:]).astype(BF16)
             dn = (acc[r, :].astype(BF16) + side).astype(F32)
             xf = x[r, :].astype(F32)
             inv = inv_s[layer, r, 0:1]
@@ -577,9 +577,9 @@
         return first_load(last, t, buf_a), pltpu.make_async_copy(rows, buf_b.at[lax.rem(t, 2)], w_sem.at[1, lax.rem(t, 2)])
 
     def fused(buf_a, buf_b, dpre, y, acc, out):
-        y[...] = jnp.zeros_like(y)
-        acc[...] = jnp.zeros_like(acc)
-        dlow[...] = jnp.zeros_like(dlow)
+        y[:] = jnp.zeros_like(y)
+        acc[:] = jnp.zeros_like(acc)
+        dlow[:] = jnp.zeros_like(dlow)
         for matrix in range(2):
             swap_own(LAYERS - 2, matrix).start()
 
@@ -616,16 +616,16 @@
                 r = pl.ds(pl.multiple_of(ROWS * h, ROWS), ROWS)
                 down = buf_b.at[slot]
                 pre = dot(u[r, :], buf_a[slot]) + dot(v6[r, :], b6[:, pl.ds(c, UP_TILE)])
-                dh = dot_t(d[r, :], down[...].reshape(UP_TILE, HIDDEN)).astype(BF16).astype(F32)
+                dh = dot_t(d[r, :], down[:].reshape(UP_TILE, HIDDEN)).astype(BF16).astype(F32)
                 s, slope = gelu_both(pre.astype(BF16))
                 dp = (dh * slope).astype(BF16)
                 dpre[r, :] = dp
-                y[r, :] += dot(s.astype(BF16), down[...].reshape(UP_TILE, HIDDEN))
+                y[r, :] += dot(s.astype(BF16), down[:].reshape(UP_TILE, HIDDEN))
                 acc[r, :] += dot_t(dp, buf_a[slot])
 
                 @pl.when(h == 1)
                 def _():
-                    low_parts(last, dpre[...], c)
+                    low_parts(last, dpre[:], c)
             return carry
 
         lax.fori_loop(FUSED_FROM, FUSED_TO, iteration, 0)
@@ -709,8 +709,8 @@
                 for load in reloads(layer):
                     load.start()
                 adapters(layer)
-                acc[...] = jnp.zeros_like(acc)
-                dlow[...] = jnp.zeros_like(dlow)
+                acc[:] = jnp.zeros_like(acc)
+                dlow[:] = jnp.zeros_like(dlow)
 
             h = n + BACK_SENT + BACK_AHEAD
             pl.when(h < 4 * SUBS)(lambda: send_back(h))
@@ -727,7 +727,7 @@
                 dp = (dh * act[s, r, :]).astype(BF16)
                 dpre[r, :] = dp
                 acc[r, :] += dot_t(dp, buf_a[s])
-            low_parts(layer, dpre[...], *fs)
+            low_parts(layer, dpre[:], *fs)
 
             @pl.when(b == steps - 1)
             def _():

time: 447 us -> 447 us (level)
  no operation moved by 1% of the time
where the time goes in v3:
time: 447 us
  Pallas kernels  440 us (98%)
  local copies, waits for them, and re-layouts  6.37 us (1%)
    pallas_call x1, Pallas kernels, step(): pl.pallas_call(step_kernel, out_shape=[o[0] for o in outs], in_specs=[any...  440 us

profile of v3, /device:TPU:0, one launch (start us, length us, event | category | flops | bytes accessed | tf_op | source)
XLA Modules:
  0.0 447.1 jit_solution(8095886423890402497)
XLA Ops:
  0.6 440.1 %mlp_stack.1 = (bf16[1024,1280]{1,0:T(8,128)(2,1)}, bf16[1024,1280]{1,0:T(8,128)(2,1)}, f32[3,4,1280]{2,1,0:T(4,128)}, f32[3,4,5120]{2,1,0:T(4,128)}, bf16[2,128...) custom-call(bf16[1024,1280]{1,0:T(8,128)(2,1)} %tokens.1, ...), custom_call_target="tpu_custom_call" | custom-call | flops 161061273600 | bytes 400000000 | tf_op jit(solution)/shard_map/mlp_stack/pallas_call | solution.py:779
  440.7 0.0 copy-start
  440.7 3.6 copy.14
  444.3 0.0 copy-done
  444.3 0.0 copy-start.2
  444.3 0.0 copy-start.1
  444.3 1.5 copy.15
  445.8 0.0 copy-done.2
  445.8 0.6 copy.16
  446.4 0.0 copy-done.1
  446.4 0.7 copy.17
Async XLA Ops:
  440.7 3.6 copy-start
  444.3 1.5 copy-start.2
  444.3 2.1 copy-start.1
